TPU v7x, 32 devices: a whole 2x2x4 slice. The times are simulated.
32 devices in a mesh: cells: 8 (over y, x, core), genes: 4 (over z).
Axes of the slice: x: 2, y: 2, z: 4, core: 2. Of those that a mesh axis runs over, the one named last changes fastest.
Arguments:
- counts: int32 [8192, 4096], P('cells', 'genes'), may hold values from 0 to 26, as said below
- library: int32 [8192], P('cells'), may hold values from 2000 to 19999
Outputs:
- adjacency: float32 [4096, 4096], P('cells', 'genes')
- connectivity: float32 [4096], P('cells')
Inputs may be any that keep to these rules, and one draw needn't show every extreme that they name: Non-negative integer counts.
All inputs are finite; a program needn't handle non-finite values.
Results may differ from a plain program's by a relative error of at most 0.006.
Values may be sent and summed in bfloat16 or wider, within the bound.
A program may use at most 128 MiB of HBM per device.

v0:
```python
import functools

import jax
import jax.numpy as jnp
from jax import lax
from jax.experimental import pallas as pl
from jax.experimental.pallas import tpu as pltpu
from jax.sharding import PartitionSpec as P

CHUNKS = 8
TILE = 512
QUARTERS = 4
UNIT = 28000.0
MESH = pl.DeviceIdType.MESH


def bit(value, index):
    return (value // (1 << index)) % 2


def flip(value, index):
    return value + (1 << index) * (1 - 2 * bit(value, index))


def planes(own, sums_ref, out_ref, conn_ref,
           sib, stat, stream, tiles, land1, land2, outn, outt, inbox,
           pstat, message, table, columns, lanes, cmsg, cin,
           stat_send, stat_recv, side_send, sib_send, sib_recv, stream_send, stream_recv, go,
           one_send, one_recv, two_send, two_recv, norm_send, turn_send, in_recv,
           sum_send, sum_recv, row_send, row_recv, conn_send, conn_recv):
    quarters, width, cells = own.shape
    block = quarters * width
    total_cells = float(cells * 8)
    c = lax.axis_index("cells")
    g = lax.axis_index("genes")
    chip = c // 2
    core = c % 2
    side = g // 2
    far = 3 * side
    near = 1 + side
    beyond = 2 - side
    farther = 3 - 3 * side
    pair = g + 1 - 2 * (g % 2)
    other = c + 1 - 2 * core
    inner = (g == 1) | (g == 2)
    outer = (g == 0) | (g == 3)
    lead = core == side
    aux = core != side

    barrier = pltpu.get_barrier_semaphore()

    @pl.loop(1, 32)
    def _(d):
        t = lax.rem(c * 4 + g + d, 32)
        pl.semaphore_signal(barrier, inc=1, device_id=(t // 4, lax.rem(t, 4)), device_id_type=MESH)

    def remote(src, dst, send, recv, device):
        return pltpu.make_async_remote_copy(
            src_ref=src, dst_ref=dst, send_sem=send, recv_sem=recv, device_id=device, device_id_type=MESH)

    def swap(q):
        return remote(own.at[q], stat.at[q], stat_send.at[q], stat_recv.at[q], (c, pair))

    def share():
        return remote(own, sib, sib_send, sib_recv, (other, g))

    def back(q):
        return remote(own.at[q], stream.at[q], side_send.at[q], stream_recv.at[q], (other, far))

    def across(q):
        return remote(own.at[q], stream.at[q], stream_send.at[q], stream_recv.at[q], (c, beyond))

    def inward(q):
        return remote(own.at[q], stream.at[4 + q], stream_send.at[q], stream_recv.at[4 + q], (c, near))

    def relay(q):
        return remote(stream.at[4 + q], stream.at[4 + q], stream_send.at[4 + q], stream_recv.at[4 + q], (c, beyond))

    def local_sums(d):
        return remote(sums_ref, pstat.at[c], sum_send.at[d], sum_recv.at[c], (lax.rem(c + d, 8), g))

    def sums_from(d):
        source = lax.rem(c + d, 8)
        return remote(sums_ref, pstat.at[source], sum_send.at[d], sum_recv.at[source], (source, g))

    def genes_to(d):
        return remote(message, table.at[g], row_send.at[d], row_recv.at[g], (c, lax.rem(g + d, 4)))

    def genes_from(d):
        source = lax.rem(g + d, 4)
        return remote(message, table.at[source], row_send.at[d], row_recv.at[source], (c, source))

    def conn_to(d):
        return remote(cmsg, cin.at[g], conn_send.at[d], conn_recv.at[g], (c, lax.rem(g + d, 4)))

    def conn_from(d):
        source = lax.rem(g + d, 4)
        return remote(cmsg, cin.at[source], conn_send.at[d], conn_recv.at[source], (c, source))

    crossing = chip // 2 != side

    @pl.when(chip // 2 == side)
    def _():
        inbox[1 - side] = jnp.zeros(inbox.shape[1:], inbox.dtype)

    pl.semaphore_wait(barrier, 31)

    for d in range(1, 8):
        local_sums(d).start()

    @pl.when(lead)
    def _():
        swap(0).start()

    @pl.when(aux)
    def _():
        share().start()

    @pl.when(aux & inner)
    def _():
        across(0).start()
        back(0).start()

    pstat[c] = sums_ref[...]
    for d in range(1, 8):
        sums_from(d).wait_recv()
    everyone = pstat[0]
    for d in range(1, 8):
        everyone = everyone + pstat[d]
    together = pstat[2 * chip] + pstat[2 * chip + 1]
    means = everyone[0:1] / total_cells
    variances = everyone[1:2] / total_cells - means * means
    scales = lax.rsqrt(variances + 1e-05)
    message[0:1] = means
    message[1:2] = scales * ((UNIT / total_cells) ** 0.5)
    message[2:3] = sums_ref[0:1]
    message[3:4] = together[0:1]
    message[4:8] = jnp.zeros((4, block), jnp.float32)
    table[g] = message[...]
    for d in range(1, 4):
        genes_to(d).start()

    @pl.when(lead)
    def _():
        for q in range(1, 4):
            swap(q).start()

    @pl.when(aux & inner)
    def _():
        for q in range(1, 4):
            across(q).start()
            back(q).start()

    @pl.when(lead & outer)
    def _():
        for q in range(4):
            swap(q).wait_send()
        pl.semaphore_signal(go, inc=1, device_id=(other, g), device_id_type=MESH)

    @pl.when(aux & outer)
    def _():
        pl.semaphore_wait(go, 1)
        for q in range(4):
            inward(q).start()

    for d in range(1, 4):
        genes_from(d).wait_recv()

    @pl.when(aux & inner)
    def _():
        for q in range(4):
            inward(q).wait_recv()
            relay(q).start()

    def first_axis(idx):
        return 1 + idx % 2

    def turn(value, step):
        return value + step * (1 - 2 * ((value // step) % 2))

    def place(piece, idx):
        one = first_axis(idx)
        two = 3 - one
        return (2 * ((piece // one + chip // one) % 2) + (piece // two + chip // two) % 2)

    def fold_one(idx):
        partner = turn(chip, first_axis(idx))
        return remote(tiles.at[idx, pl.ds(2, 2)], land1.at[idx], one_send.at[idx], one_recv.at[idx],
                      (2 * partner + core, g))

    def fold_two(idx):
        partner = turn(chip, 3 - first_axis(idx))
        return remote(tiles.at[idx, 1], land2.at[idx], two_send.at[idx], two_recv.at[idx],
                      (2 * partner + core, g))

    def where(test, yes, no):
        return jnp.where(test, yes, no)

    late = lambda idx: (idx - 8) // 3
    phase = lambda idx: (idx - 8) % 3

    def rows_of(idx):
        crossed = where(idx < 8, beyond, where(phase(idx) == 0, beyond, farther))
        return where(inner, where(idx < 4, near, crossed), far)

    def quarter_of(idx):
        return where(inner & (idx >= 8), late(idx), idx % 4)

    def cols_of(idx):
        crossed = where(idx < 8, near, where(phase(idx) == 1, near, far))
        return where(inner, where(idx < 4, near, crossed), where(idx < 4, far, near))

    def normal(idx):
        q = quarter_of(idx)
        return remote(outn.at[idx], inbox.at[side, q % 2, chip], norm_send.at[idx], in_recv.at[side, q % 2, chip],
                      (2 * rows_of(idx) + q // 2, cols_of(idx)))

    def turned(idx):
        q = quarter_of(idx)
        return remote(outt.at[idx], inbox.at[side, chip % 2, q], turn_send.at[idx], in_recv.at[side, chip % 2, q],
                      (2 * cols_of(idx) + chip // 2, rows_of(idx)))

    def normal_here(idx):
        return (2 * rows_of(idx) + quarter_of(idx) // 2 == c) & (cols_of(idx) == g)

    def turned_here(idx):
        return (2 * cols_of(idx) + chip // 2 == c) & (rows_of(idx) == g)

    def absorb_one(idx):
        fold_one(idx).wait_recv()
        tiles[idx, 1] = (tiles[idx, 1].astype(jnp.int32) + land1[idx, 1].astype(jnp.int32)).astype(jnp.int16)
        fold_two(idx).start()

    def absorb_two(idx):
        fold_two(idx).wait_recv()
        total = (tiles[idx, 0].astype(jnp.int32) + land1[idx, 0].astype(jnp.int32)
                 + land2[idx].astype(jnp.int32))
        q = quarter_of(idx)
        here = normal_here(idx)

        @pl.when(here)
        def _():
            inbox[side, q % 2, chip] = total.astype(jnp.int16)

        @pl.when(jnp.logical_not(here))
        def _():
            outn[idx] = total.astype(jnp.int16)
            normal(idx).start()

        @pl.when(rows_of(idx) != cols_of(idx))
        def _():
            across_total = jnp.transpose(total)
            self_turned = turned_here(idx)

            @pl.when(self_turned)
            def _():
                inbox[side, chip % 2, q] = across_total.astype(jnp.int16)

            @pl.when(jnp.logical_not(self_turned))
            def _():
                outt[idx] = across_total.astype(jnp.int16)
                turned(idx).start()

    def product(idx, row, count, parts):
        row_block = rows_of(idx)
        col_block = cols_of(idx)
        first = pl.multiple_of(quarter_of(idx) * width, width)
        stats = columns[row_block, pl.ds(first, width), :]
        scale_j = stats[:, 1:2]
        mean_j = scale_j * stats[:, 0:1]
        sum_j = scale_j * stats[:, row:row + 1]

        @pl.loop(0, quarters)
        def _(p):
            acc = 0.0
            for left, right in parts:
                acc = acc + lax.dot_general(left[...], right(p)[...], (((1,), (1,)), ((), ())),
                                            preferred_element_type=jnp.float32)
            span = pl.ds(pl.multiple_of(p * width, width), width)
            mean_i = table[col_block, 0:1, span]
            scale_i = table[col_block, 1:2, span]
            drift_i = table[col_block, row:row + 1, span] - count * mean_i
            value = (acc * scale_j - mean_j * drift_i - sum_j * mean_i) * scale_i
            tiles[idx, place(p, idx)] = jnp.round(value).astype(jnp.int32).astype(jnp.int16)

    tasks = where(inner, 20, 8)

    @pl.when(lead)
    def _():
        for z in range(4):
            columns[z] = jnp.transpose(table[z])
        share().wait_recv()

        @pl.loop(0, tasks)
        def _(idx):
            q = quarter_of(idx)

            @pl.when(idx < 4)
            def _():
                product(idx, 3, 2.0 * cells,
                        [(own.at[q], lambda p: own.at[p]), (sib.at[q], lambda p: sib.at[p])])

            @pl.when(outer & (idx >= 4))
            def _():
                @pl.when(idx == 4)
                def _():
                    for t in range(4):
                        swap(t).wait_recv()
                        back(t).wait_recv()
                product(idx, 3, 2.0 * cells,
                        [(own.at[q], lambda p: stat.at[p]), (sib.at[q], lambda p: stream.at[p])])

            @pl.when(inner & (idx >= 4))
            def _():
                arriving = where(idx < 8, idx - 4, 4 + late(idx))
                waits = (idx < 8) | (phase(idx) == 1)

                @pl.when(waits)
                def _():
                    remote(own.at[0], stream.at[arriving], stream_send.at[arriving], stream_recv.at[arriving],
                           (c, beyond)).wait_recv()
                    product(idx, 2, 1.0 * cells, [(stream.at[arriving], lambda p: own.at[p])])

                @pl.when(jnp.logical_not(waits))
                def _():
                    @pl.when(idx == 8)
                    def _():
                        for t in range(4):
                            swap(t).wait_recv()
                    held = where(phase(idx) == 0, late(idx), 4 + late(idx))
                    product(idx, 2, 1.0 * cells, [(stream.at[held], lambda p: stat.at[p])])

            fold_one(idx).start()

            @pl.when(idx >= 1)
            def _():
                absorb_one(idx - 1)

            @pl.when(idx >= 2)
            def _():
                absorb_two(idx - 2)

        absorb_one(tasks - 1)
        absorb_two(tasks - 2)
        absorb_two(tasks - 1)

    lanes[...] = jnp.zeros_like(lanes)
    height = 2 * width

    @pl.loop(0, 8)
    def _(n):
        piece = n // 2
        r = n % 2
        mine = jnp.where(crossing, inner & (chip == piece),
                         jnp.where(chip == g, chip == piece, outer & (chip == 2 * core + r)))

        @pl.when(jnp.logical_not(mine & lead))
        def _():
            remote(outn.at[0], inbox.at[side, r, piece], norm_send.at[0], in_recv.at[side, r, piece],
                   (other, g)).wait_recv()

        @pl.when(crossing)
        def _():
            remote(outn.at[0], inbox.at[1 - side, r, piece], norm_send.at[0], in_recv.at[1 - side, r, piece],
                   (other, g)).wait_recv()
        total = inbox[0, r, piece].astype(jnp.int32) + inbox[1, r, piece].astype(jnp.int32)
        value = total.astype(jnp.float32) * (1.0 / UNIT)
        square = value * value
        powered = square * square * square
        rows = c * height + r * width + lax.broadcasted_iota(jnp.int32, (width, width), 0)
        cols = g * block + piece * width + lax.broadcasted_iota(jnp.int32, (width, width), 1)
        powered = jnp.where(rows == cols, 0.0, powered)
        down = pl.ds(pl.multiple_of(r * width, width), width)
        out_ref[down, pl.ds(pl.multiple_of(piece * width, width), width)] = powered
        part = powered[:, 0:128]
        for lane in range(1, width // 128):
            part = part + powered[:, lane * 128:(lane + 1) * 128]
        lanes[down, :] = lanes[down, :] + part

    cmsg[...] = jnp.broadcast_to(jnp.sum(jnp.transpose(lanes[...]), axis=0, keepdims=True), cmsg.shape)
    for d in range(1, 4):
        conn_to(d).start()
    cin[g] = cmsg[...]
    for d in range(1, 4):
        conn_from(d).wait_recv()
    conn_ref[...] = (cin[0] + cin[1]) + (cin[2] + cin[3])

    for d in range(1, 8):
        local_sums(d).wait_send()
    for d in range(1, 4):
        genes_to(d).wait_send()
        conn_to(d).wait_send()

    @pl.when(aux)
    def _():
        share().wait_send()

    @pl.when(aux & inner)
    def _():
        for q in range(4):
            across(q).wait_send()
            back(q).wait_send()
            relay(q).wait_send()

    @pl.when(aux & outer)
    def _():
        for q in range(4):
            inward(q).wait_send()

    @pl.when(lead & inner)
    def _():
        for q in range(4):
            swap(q).wait_send()

    @pl.when(lead)
    def _():
        @pl.loop(0, tasks)
        def _(idx):
            fold_one(idx).wait_send()
            fold_two(idx).wait_send()

            @pl.when(jnp.logical_not(normal_here(idx)))
            def _():
                normal(idx).wait_send()

            @pl.when((rows_of(idx) != cols_of(idx)) & jnp.logical_not(turned_here(idx)))
            def _():
                turned(idx).wait_send()


def by_planes(counts, library):
    factor = 10000.0 / library.astype(jnp.float32)
    expressed = jnp.log1p(counts.astype(jnp.float32) * factor[:, None])
    expressed = lax.reduce_precision(expressed, 8, 7)
    cells, block = expressed.shape
    width = block // QUARTERS
    sums = jnp.stack([jnp.sum(expressed, axis=0), jnp.sum(expressed * expressed, axis=0)])
    sums = jnp.concatenate([sums, jnp.zeros((6, block), jnp.float32)], axis=0)
    own = expressed.astype(jnp.bfloat16).T.reshape(QUARTERS, width, cells)
    vmem = pl.BlockSpec(memory_space=pltpu.VMEM)
    dma = pltpu.SemaphoreType.DMA
    small = jnp.int16
    count = 20
    adjacency, connectivity = pl.pallas_call(
        planes,
        out_shape=(
            jax.ShapeDtypeStruct((2 * width, block), jnp.float32),
            jax.ShapeDtypeStruct((8, 2 * width), jnp.float32),
        ),
        in_specs=[vmem] * 2,
        out_specs=(vmem, vmem),
        scratch_shapes=[
            pltpu.VMEM((QUARTERS, width, cells), jnp.bfloat16),
            pltpu.VMEM((QUARTERS, width, cells), jnp.bfloat16),
            pltpu.VMEM((8, width, cells), jnp.bfloat16),
            pltpu.VMEM((count, 4, width, width), small),
            pltpu.VMEM((count, 2, width, width), small),
            pltpu.VMEM((count, width, width), small),
            pltpu.VMEM((count, width, width), small),
            pltpu.VMEM((count, width, width), small),
            pltpu.VMEM((2, 2, 4, width, width), small),
            pltpu.VMEM((8, 8, block), jnp.float32),
            pltpu.VMEM((8, block), jnp.float32),
            pltpu.VMEM((4, 8, block), jnp.float32),
            pltpu.VMEM((4, block, 8), jnp.float32),
            pltpu.VMEM((2 * width, 128), jnp.float32),
            pltpu.VMEM((8, 2 * width), jnp.float32),
            pltpu.VMEM((4, 8, 2 * width), jnp.float32),
            dma((4,)), dma((4,)), dma((4,)), dma, dma, dma((8,)), dma((8,)), pltpu.SemaphoreType.REGULAR,
            dma((count,)), dma((count,)), dma((count,)), dma((count,)), dma((count,)), dma((count,)), dma((2, 2, 4)),
            dma((8,)), dma((8,)), dma((4,)), dma((4,)), dma((4,)), dma((4,)),
        ],
        compiler_params=pltpu.CompilerParams(
            collective_id=1, has_side_effects=True, vmem_limit_bytes=58 * 1024 * 1024),
    )(own, sums)
    return adjacency, connectivity[0]


def network(cell_groups, gene_groups, xq_ref, own_ref, sums_ref, out_ref, stats_ref,
            held, partial, landed, totals, sums_in,
            ring_send, ring_recv, cut_send, cut_recv, fly_send, fly_recv, stat_send, stat_recv):
    owners, chunks, part, cells = xq_ref.shape
    rows = owners * part
    cols = own_ref.shape[1]
    half = cols // 2
    c = lax.axis_index("cells")
    g = lax.axis_index("genes")
    right = lax.rem(g + 1, gene_groups)
    left = lax.rem(g + gene_groups - 1, gene_groups)
    bits = cell_groups.bit_length() - 1
    hops = gene_groups - 1
    orders = (tuple(range(bits)), (0,) + tuple(range(bits - 1, 0, -1)))

    barrier = pltpu.get_barrier_semaphore()
    for target in [(c, left), (c, right)] + [(flip(c, b), g) for b in range(bits)]:
        pl.semaphore_signal(barrier, inc=1, device_id=target, device_id_type=pl.DeviceIdType.MESH)
    pl.semaphore_wait(barrier, 2 + bits)

    def ring(q, hop, piece):
        span = pl.ds(piece * (owners // 2), owners // 2)
        source = xq_ref.at[span, q] if hop == 0 else held.at[q, hop - 1, span]
        return pltpu.make_async_remote_copy(
            src_ref=source, dst_ref=held.at[q, hop, span],
            send_sem=ring_send.at[q, hop, piece], recv_sem=ring_recv.at[q, hop, piece],
            device_id=(c, right), device_id_type=pl.DeviceIdType.MESH)

    def cut(q, side, stage):
        count = cell_groups >> (stage + 1)
        return pltpu.make_async_remote_copy(
            src_ref=partial.at[q, side, pl.ds(count, count)],
            dst_ref=landed.at[q, side, pl.ds(count, count)],
            send_sem=cut_send.at[q, side, stage], recv_sem=cut_recv.at[q, side, stage],
            device_id=(flip(c, orders[side][stage]), g), device_id_type=pl.DeviceIdType.MESH)

    def fly(stage):
        return pltpu.make_async_remote_copy(
            src_ref=totals.at[stage], dst_ref=sums_in.at[stage],
            send_sem=fly_send.at[stage], recv_sem=fly_recv.at[stage],
            device_id=(flip(c, stage), g), device_id_type=pl.DeviceIdType.MESH)

    def spread(hop):
        source = totals.at[bits] if hop == 0 else stats_ref.at[hop]
        return pltpu.make_async_remote_copy(
            src_ref=source, dst_ref=stats_ref.at[hop + 1],
            send_sem=stat_send.at[hop], recv_sem=stat_recv.at[hop],
            device_id=(c, right), device_id_type=pl.DeviceIdType.MESH)

    def place(owner, side):
        total = 0
        for position, b in enumerate(orders[side]):
            total = total + ((bit(owner, b) + bit(c, b)) % 2) * (1 << (bits - 1 - position))
        return total

    def multiply(q, step):
        source = lax.rem(g - step + gene_groups, gene_groups)
        block = xq_ref.at[:, q] if step == 0 else held.at[q, step - 1]
        for side in range(2):
            spots = [place(source * owners + o, side) for o in range(owners)]

            @pl.loop(0, half // TILE)
            def _(t):
                start = pl.multiple_of(t * TILE, TILE)
                columns = pl.ds(pl.multiple_of(side * half + start, TILE), TILE)
                tile = jnp.dot(block[...].reshape(rows, cells), own_ref[:, columns], preferred_element_type=jnp.float32)
                for o in range(owners):
                    partial[q, side, spots[o], :, pl.ds(start, TILE)] = tile[o * part:(o + 1) * part]

    def launch(q, stage):
        for side in range(2):
            cut(q, side, stage).start()

    def absorb(q, stage):
        count = cell_groups >> (stage + 1)
        for side in range(2):
            cut(q, side, stage).wait_recv()
            if count > 1:
                @pl.loop(0, count)
                def _(i):
                    partial[q, side, i] = partial[q, side, i] + landed[q, side, i + count]
            else:
                out_ref[pl.ds(q * part, part), side * half:(side + 1) * half] = (
                    partial[q, side, 0] + landed[q, side, 1])

    for piece in range(2):
        ring(0, 0, piece).start()
    totals[0] = sums_ref[...]
    for stage in range(bits):
        fly(stage).start()
        fly(stage).wait_recv()
        totals[stage + 1] = totals[stage] + sums_in[stage]
    stats_ref[0] = totals[bits]

    turns = [[s for s in range(bits) if s * hops // bits == h] for h in range(hops)]

    @pl.loop(0, chunks)
    def _(q):
        multiply(q, 0)
        for hop in range(hops):
            for piece in range(2):
                ring(q, hop, piece).wait_recv()
                if hop < hops - 1:
                    ring(q, hop + 1, piece).start()
            if hop == max(hops - 2, 0):
                @pl.when(q < chunks - 1)
                def _():
                    for piece in range(2):
                        ring(q + 1, 0, piece).start()

            @pl.when(q > 0)
            def _():
                for stage in turns[hop]:
                    absorb(q - 1, stage)
                    if stage + 1 < bits:
                        launch(q - 1, stage + 1)
            multiply(q, hop + 1)
        launch(q, 0)

    last = chunks - 1
    spread(0).start()
    for stage in range(bits):
        absorb(last, stage)
        if stage + 1 < bits:
            launch(last, stage + 1)
        if stage < hops:
            spread(stage).wait_recv()
            if stage + 1 < hops:
                spread(stage + 1).start()
    for hop in range(bits, hops):
        spread(hop).wait_recv()
        if hop + 1 < hops:
            spread(hop + 1).start()
    for hop in range(hops):
        spread(hop).wait_send()
    for stage in range(bits):
        fly(stage).wait_send()

    @pl.loop(0, chunks)
    def _(q):
        for hop in range(hops):
            for piece in range(2):
                ring(q, hop, piece).wait_send()
        for side in range(2):
            for stage in range(bits):
                cut(q, side, stage).wait_send()


def normalize(counts, library):
    factor = 10000.0 / library.astype(jnp.float32)
    return jnp.log1p(counts.astype(jnp.float32) * factor[:, None]).astype(jnp.bfloat16)


def shards(counts, library):
    own_block = normalize(counts, library)
    cells, col_width = own_block.shape
    cell_groups = lax.axis_size("cells")
    gene_groups = lax.axis_size("genes")
    row_width = col_width * gene_groups // cell_groups
    owners = col_width // row_width
    total_cells = float(cells * cell_groups)
    me = lax.axis_index("genes")

    chunks = min(CHUNKS, row_width // 16)
    part = row_width // chunks
    ordered = own_block.T.reshape(owners, chunks, part, cells)
    widened = own_block.astype(jnp.float32)
    sums = jnp.stack([jnp.sum(widened, axis=0), jnp.sum(widened * widened, axis=0)])
    sums = jnp.concatenate([sums, jnp.zeros((6, col_width), jnp.float32)], axis=0)
    bits = cell_groups.bit_length() - 1
    hops = gene_groups - 1
    vmem = pl.BlockSpec(memory_space=pltpu.VMEM)
    dma = pltpu.SemaphoreType.DMA
    gram_tile, stats = pl.pallas_call(
        functools.partial(network, cell_groups, gene_groups),
        out_shape=(
            jax.ShapeDtypeStruct((row_width, col_width), jnp.float32),
            jax.ShapeDtypeStruct((gene_groups, 8, col_width), jnp.float32),
        ),
        in_specs=[vmem] * 3,
        out_specs=(vmem, vmem),
        scratch_shapes=[
            pltpu.VMEM((chunks, hops, owners, part, cells), jnp.bfloat16),
            pltpu.VMEM((chunks, 2, cell_groups, part, col_width // 2), jnp.float32),
            pltpu.VMEM((chunks, 2, cell_groups, part, col_width // 2), jnp.float32),
            pltpu.VMEM((bits + 1, 8, col_width), jnp.float32),
            pltpu.VMEM((bits, 8, col_width), jnp.float32),
            dma((chunks, hops, 2)), dma((chunks, hops, 2)),
            dma((chunks, 2, bits)), dma((chunks, 2, bits)),
            dma((bits,)), dma((bits,)),
            dma((hops,)), dma((hops,)),
        ],
        compiler_params=pltpu.CompilerParams(
            collective_id=0, has_side_effects=True, vmem_limit_bytes=60 * 1024 * 1024),
    )(ordered, own_block, sums)
    order = lax.rem(me - jnp.arange(gene_groups) + gene_groups, gene_groups)
    all_sums = jnp.transpose(jnp.take(stats[:, :2], order, axis=0), (1, 0, 2)).reshape(2, -1)

    means = all_sums[0] / total_cells
    variances = all_sums[1] / total_cells - means * means
    scales = lax.rsqrt(variances + 1e-05)
    row_first = lax.axis_index("cells") * row_width
    col_first = me * col_width
    row_means = lax.dynamic_slice_in_dim(means, row_first, row_width, 0)
    col_means = lax.dynamic_slice_in_dim(means, col_first, col_width, 0)
    row_scales = lax.dynamic_slice_in_dim(scales, row_first, row_width, 0)
    col_scales = lax.dynamic_slice_in_dim(scales, col_first, col_width, 0)
    correlation = (
        (gram_tile / total_cells - row_means[:, None] * col_means[None, :])
        * row_scales[:, None]
        * col_scales[None, :]
    )
    powered = correlation**6
    row_index = row_first + jnp.arange(row_width, dtype=jnp.int32)[:, None]
    col_index = col_first + jnp.arange(col_width, dtype=jnp.int32)[None, :]
    adjacency = jnp.where(row_index == col_index, jnp.float32(0.0), powered)
    connectivity = lax.psum(jnp.sum(adjacency, axis=1), "genes")
    return (adjacency, connectivity)


def solution(mesh):
    sized = mesh.shape["genes"] == 4 and mesh.shape["cells"] == 8
    return jax.shard_map(
        by_planes if sized else shards,
        mesh=mesh,
        in_specs=(P("cells", "genes"), P("cells")),
        out_specs=(P("cells", "genes"), P("cells")),
        check_vma=False,
    )
```

profile of v0, /device:TPU:1, one launch (start us, length us, event | category | flops | bytes accessed | tf_op | source)
XLA Modules:
  0.0 154.6 jit_solution(14224157278068254250)
XLA Ops:
  0.6 0.1 pad.2.clone
  0.7 0.7 convert_divide_fusion
  1.4 4.4 %fusion = (f32[1024]{0:T(1024)S(1)}, f32[1024]{0:T(1024)S(1)}, bf16[1024,1024]{0,1:T(8,128)(2,1)S(1)}) fusion(s32[1024,1024]{1,0:T(8,128)} %param.2, f32[1024]{0:T(1024)S(1)} %convert_divide_fusion), kind=kLoop, calls=%fused_computation.2 | loop fusion | flops 7337984 | bytes 6303744 | tf_op jit(solution)/shard_map/reduce_sum | solution.py:437
  5.8 0.7 maximum_maximum_fusion.sums_ref
  6.5 2.5 %copy.4 = bf16[1024,1024]{1,0:T(8,128)(2,1)} copy(bf16[1024,1024]{0,1:T(8,128)(2,1)S(1)} %get-tuple-element.8) | data formatting | bytes 4194304 | tf_op jit(solution)/shard_map/transpose | solution.py:439
  9.0 141.1 %shard_map.41 = (f32[512,1024]{1,0:T(8,128)}, f32[8,512]{1,0:T(8,128)}) custom-call(bf16[4,256,1024]{2,1,0:T(8,128)(2,1)} %bitcast.6, f32[8,1024]{1,0:T(8,128)} %maximum_maximum_fusion.sums_ref), custom_call_target="tpu_custom_call" | custom-call | tf_op jit(solution)/shard_map/pallas_call | solution.py:444
  150.2 1.3 slice.3
  151.5 3.2 %copy.6 = f32[512,1024]{1,0:T(8,128)} copy(f32[512,1024]{1,0:T(8,128)} %get-tuple-element.11) | data formatting | bytes 4194304
  (1 shorter events, 0.0 us)
where the time goes:
time: 155 us
  Pallas kernels  141 us (91%)
  local copies, waits for them, and re-layouts  7.07 us (5%)
  other arithmetic  5.75 us (4%)
    pallas_call x1, Pallas kernels, by_planes(): pl.pallas_call(planes, out_shape=(jax.ShapeDtypeStruct((2 * width, block)...  141 us
    reduce_sum x1, other arithmetic, by_planes(): jnp.sum(expressed, axis=0)  4.39 us
    unnamed x1, local copies, waits for them, and re-layouts  3.16 us

commit v1 on v0

--- a/solution.py
+++ b/solution.py
@@ -11,6 +11,9 @@
 TILE = 512
 QUARTERS = 4
 UNIT = 28000.0
+LAG_ONE = 3
+LAG_TWO = 5
+GO_AT = 6
 MESH = pl.DeviceIdType.MESH
 
 
@@ -22,14 +25,13 @@
     return value + (1 << index) * (1 - 2 * bit(value, index))
 
 
-def planes(own, sums_ref, out_ref, conn_ref,
-           sib, stat, stream, tiles, land1, land2, outn, outt, inbox,
+def planes(counts_ref, library_ref, out_ref, conn_ref,
+           raw, own, sums_ref, squares, result, sib, stat, held, stream, tiles, land1, land2, whole, outn, outt, inbox,
            pstat, message, table, columns, lanes, cmsg, cin,
-           stat_send, stat_recv, side_send, sib_send, sib_recv, stream_send, stream_recv, go,
-           one_send, one_recv, two_send, two_recv, norm_send, turn_send, in_recv,
-           sum_send, sum_recv, row_send, row_recv, conn_send, conn_recv):
+           stat_send, stat_recv, held_send, held_recv, sib_send, sib_recv, stream_send, stream_recv, go,
+           one_send, one_recv, two_send, two_recv, hand_send, hand_recv, norm_send, turn_send, in_recv,
+           load_done, store_done, sum_send, sum_recv, row_send, row_recv, conn_send, conn_recv):
     quarters, width, cells = own.shape
-    block = quarters * width
     total_cells = float(cells * 8)
     c = lax.axis_index("cells")
     g = lax.axis_index("genes")
@@ -40,7 +42,6 @@
     near = 1 + side
     beyond = 2 - side
     farther = 3 - 3 * side
-    pair = g + 1 - 2 * (g % 2)
     other = c + 1 - 2 * core
     inner = (g == 1) | (g == 2)
     outer = (g == 0) | (g == 3)
@@ -54,19 +55,42 @@
         t = lax.rem(c * 4 + g + d, 32)
         pl.semaphore_signal(barrier, inc=1, device_id=(t // 4, lax.rem(t, 4)), device_id_type=MESH)
 
+    slabs, slab, block = raw.shape
+
+    def load(r):
+        return pltpu.make_async_copy(counts_ref.at[pl.ds(r * slab, slab)], raw.at[r], load_done.at[r])
+
+    @pl.loop(0, slabs)
+    def _(r):
+        load(r).start()
+
+    sums_ref[...] = jnp.zeros_like(sums_ref)
+    squares[...] = jnp.zeros_like(squares)
+
+    @pl.loop(0, slabs)
+    def _(r):
+        load(r).wait()
+        factor = 10000.0 / library_ref[pl.ds(r, 1), :].astype(jnp.float32)
+        factor = jnp.transpose(jnp.broadcast_to(factor, (8, slab)))[:, 0:1]
+        expressed = jnp.log1p(raw[r].astype(jnp.float32) * factor).astype(jnp.bfloat16).astype(jnp.float32)
+        sums_ref[...] = sums_ref[...] + jnp.sum(expressed.reshape(slab // 8, 8, block), axis=0)
+        squares[...] = squares[...] + jnp.sum((expressed * expressed).reshape(slab // 8, 8, block), axis=0)
+        turned_slab = jnp.transpose(expressed).astype(jnp.bfloat16).reshape(quarters, width, slab)
+        own[:, :, pl.ds(pl.multiple_of(r * slab, slab), slab)] = turned_slab
+
+    total_sum = jnp.sum(sums_ref[...], axis=0, keepdims=True)
+    total_square = jnp.sum(squares[...], axis=0, keepdims=True)
+    sums_ref[...] = jnp.zeros_like(sums_ref)
+    sums_ref[0:1] = total_sum
+    sums_ref[1:2] = total_square
+
     def remote(src, dst, send, recv, device):
         return pltpu.make_async_remote_copy(
             src_ref=src, dst_ref=dst, send_sem=send, recv_sem=recv, device_id=device, device_id_type=MESH)
 
-    def swap(q):
-        return remote(own.at[q], stat.at[q], stat_send.at[q], stat_recv.at[q], (c, pair))
-
     def share():
         return remote(own, sib, sib_send, sib_recv, (other, g))
 
-    def back(q):
-        return remote(own.at[q], stream.at[q], side_send.at[q], stream_recv.at[q], (other, far))
-
     def across(q):
         return remote(own.at[q], stream.at[q], stream_send.at[q], stream_recv.at[q], (c, beyond))
 
@@ -75,6 +99,15 @@
 
     def relay(q):
         return remote(stream.at[4 + q], stream.at[4 + q], stream_send.at[4 + q], stream_recv.at[4 + q], (c, beyond))
+
+    def beside(q):
+        return remote(stream.at[4 + q], held.at[q], held_send.at[q], held_recv.at[q], (other, g))
+
+    def onward(t):
+        return remote(stream.at[t], stream.at[t], stream_send.at[t], stream_recv.at[t], (c, far))
+
+    def swap(q):
+        return remote(own.at[q], stat.at[q], stat_send.at[q], stat_recv.at[q], (c, near))
 
     def local_sums(d):
         return remote(sums_ref, pstat.at[c], sum_send.at[d], sum_recv.at[c], (lax.rem(c + d, 8), g))
@@ -108,18 +141,17 @@
     for d in range(1, 8):
         local_sums(d).start()
 
-    @pl.when(lead)
-    def _():
-        swap(0).start()
+    @pl.when(aux & inner)
+    def _():
+        across(0).start()
+
+    @pl.when(aux & outer)
+    def _():
+        inward(0).start()
 
     @pl.when(aux)
     def _():
         share().start()
-
-    @pl.when(aux & inner)
-    def _():
-        across(0).start()
-        back(0).start()
 
     pstat[c] = sums_ref[...]
     for d in range(1, 8):
@@ -140,40 +172,33 @@
     for d in range(1, 4):
         genes_to(d).start()
 
-    @pl.when(lead)
-    def _():
-        for q in range(1, 4):
-            swap(q).start()
-
     @pl.when(aux & inner)
     def _():
         for q in range(1, 4):
             across(q).start()
-            back(q).start()
-
-    @pl.when(lead & outer)
-    def _():
-        for q in range(4):
-            swap(q).wait_send()
-        pl.semaphore_signal(go, inc=1, device_id=(other, g), device_id_type=MESH)
-
-    @pl.when(aux & outer)
-    def _():
-        pl.semaphore_wait(go, 1)
-        for q in range(4):
-            inward(q).start()
-
-    for d in range(1, 4):
-        genes_from(d).wait_recv()
-
-    @pl.when(aux & inner)
-    def _():
         for q in range(4):
             inward(q).wait_recv()
             relay(q).start()
+            beside(q).start()
+
+    @pl.when(aux & outer)
+    def _():
+        for q in range(1, 4):
+            inward(q).start()
+        for q in range(4):
+            inward(q).wait_send()
+        pl.semaphore_signal(go, inc=1, device_id=(other, g), device_id_type=MESH)
+
+    @pl.when(aux)
+    def _():
+        for d in range(1, 4):
+            genes_from(d).wait_recv()
+
+    def where(test, yes, no):
+        return jnp.where(test, yes, no)
 
     def first_axis(idx):
-        return 1 + idx % 2
+        return 1 + 0 * idx
 
     def turn(value, step):
         return value + step * (1 - 2 * ((value // step) % 2))
@@ -193,38 +218,25 @@
         return remote(tiles.at[idx, 1], land2.at[idx], two_send.at[idx], two_recv.at[idx],
                       (2 * partner + core, g))
 
-    def where(test, yes, no):
-        return jnp.where(test, yes, no)
-
-    late = lambda idx: (idx - 8) // 3
-    phase = lambda idx: (idx - 8) % 3
-
     def rows_of(idx):
-        crossed = where(idx < 8, beyond, where(phase(idx) == 0, beyond, farther))
-        return where(inner, where(idx < 4, near, crossed), far)
-
-    def quarter_of(idx):
-        return where(inner & (idx >= 8), late(idx), idx % 4)
-
-    def cols_of(idx):
-        crossed = where(idx < 8, near, where(phase(idx) == 1, near, far))
-        return where(inner, where(idx < 4, near, crossed), where(idx < 4, far, near))
+        crossed = where(idx < 8, beyond, where(idx < 12, farther, far))
+        return where(idx < 4, g, crossed)
+
+    def hand(idx):
+        return remote(whole.at[idx], outn.at[idx], hand_send.at[idx], hand_recv.at[idx], (other, g))
 
     def normal(idx):
-        q = quarter_of(idx)
+        q = idx % 4
         return remote(outn.at[idx], inbox.at[side, q % 2, chip], norm_send.at[idx], in_recv.at[side, q % 2, chip],
-                      (2 * rows_of(idx) + q // 2, cols_of(idx)))
+                      (2 * rows_of(idx) + q // 2, g))
 
     def turned(idx):
-        q = quarter_of(idx)
+        q = idx % 4
         return remote(outt.at[idx], inbox.at[side, chip % 2, q], turn_send.at[idx], in_recv.at[side, chip % 2, q],
-                      (2 * cols_of(idx) + chip // 2, rows_of(idx)))
+                      (2 * g + chip // 2, rows_of(idx)))
 
     def normal_here(idx):
-        return (2 * rows_of(idx) + quarter_of(idx) // 2 == c) & (cols_of(idx) == g)
-
-    def turned_here(idx):
-        return (2 * cols_of(idx) + chip // 2 == c) & (rows_of(idx) == g)
+        return 2 * rows_of(idx) + (idx % 4) // 2 == c
 
     def absorb_one(idx):
         fold_one(idx).wait_recv()
@@ -235,36 +247,31 @@
         fold_two(idx).wait_recv()
         total = (tiles[idx, 0].astype(jnp.int32) + land1[idx, 0].astype(jnp.int32)
                  + land2[idx].astype(jnp.int32))
-        q = quarter_of(idx)
+        whole[idx] = total.astype(jnp.int16)
+        hand(idx).start()
+
+    def deliver(idx):
+        hand(idx).wait_recv()
+        q = idx % 4
         here = normal_here(idx)
 
         @pl.when(here)
         def _():
-            inbox[side, q % 2, chip] = total.astype(jnp.int16)
+            inbox[side, q % 2, chip] = outn[idx]
 
         @pl.when(jnp.logical_not(here))
         def _():
-            outn[idx] = total.astype(jnp.int16)
             normal(idx).start()
 
-        @pl.when(rows_of(idx) != cols_of(idx))
-        def _():
-            across_total = jnp.transpose(total)
-            self_turned = turned_here(idx)
-
-            @pl.when(self_turned)
-            def _():
-                inbox[side, chip % 2, q] = across_total.astype(jnp.int16)
-
-            @pl.when(jnp.logical_not(self_turned))
-            def _():
-                outt[idx] = across_total.astype(jnp.int16)
-                turned(idx).start()
+        @pl.when(idx >= 4)
+        def _():
+            outt[idx] = jnp.transpose(outn[idx].astype(jnp.int32)).astype(jnp.int16)
+            turned(idx).start()
 
     def product(idx, row, count, parts):
         row_block = rows_of(idx)
-        col_block = cols_of(idx)
-        first = pl.multiple_of(quarter_of(idx) * width, width)
+        col_block = g
+        first = pl.multiple_of((idx % 4) * width, width)
         stats = columns[row_block, pl.ds(first, width), :]
         scale_j = stats[:, 1:2]
         mean_j = scale_j * stats[:, 0:1]
@@ -283,66 +290,75 @@
             value = (acc * scale_j - mean_j * drift_i - sum_j * mean_i) * scale_i
             tiles[idx, place(p, idx)] = jnp.round(value).astype(jnp.int32).astype(jnp.int16)
 
-    tasks = where(inner, 20, 8)
+    tasks = where(inner, 16, 12)
+
+    def step(idx):
+        q = idx % 4
+
+        @pl.when(idx == 4)
+        def _():
+            for d in range(1, 4):
+                genes_from(d).wait_recv()
+                z = lax.rem(g + d, 4)
+                columns[z] = jnp.transpose(table[z])
+
+        @pl.when(outer & (idx == GO_AT))
+        def _():
+            pl.semaphore_wait(go, 1)
+            for t in range(4):
+                swap(t).start()
+
+        @pl.when(idx < 4)
+        def _():
+            product(idx, 3, 2.0 * cells,
+                    [(own.at[q], lambda p: own.at[p]), (sib.at[q], lambda p: sib.at[p])])
+
+        @pl.when((idx >= 4) & (idx < 12))
+        def _():
+            slot = idx - 4
+            remote(own.at[0], stream.at[slot], stream_send.at[slot], stream_recv.at[slot], (c, beyond)).wait_recv()
+
+            @pl.when(inner)
+            def _():
+                onward(slot).start()
+            product(idx, 2, 1.0 * cells, [(stream.at[slot], lambda p: own.at[p])])
+
+        @pl.when(idx >= 12)
+        def _():
+            swap(q).wait_recv()
+            beside(q).wait_recv()
+            product(idx, 3, 2.0 * cells,
+                    [(stat.at[q], lambda p: own.at[p]), (held.at[q], lambda p: sib.at[p])])
+
+        fold_one(idx).start()
 
     @pl.when(lead)
     def _():
-        for z in range(4):
-            columns[z] = jnp.transpose(table[z])
+        columns[g] = jnp.transpose(table[g])
         share().wait_recv()
 
-        @pl.loop(0, tasks)
+        @pl.loop(0, tasks + LAG_TWO)
         def _(idx):
-            q = quarter_of(idx)
-
-            @pl.when(idx < 4)
+            @pl.when(idx < tasks)
             def _():
-                product(idx, 3, 2.0 * cells,
-                        [(own.at[q], lambda p: own.at[p]), (sib.at[q], lambda p: sib.at[p])])
-
-            @pl.when(outer & (idx >= 4))
+                step(idx)
+
+            @pl.when((idx >= LAG_ONE) & (idx < tasks + LAG_ONE))
             def _():
-                @pl.when(idx == 4)
-                def _():
-                    for t in range(4):
-                        swap(t).wait_recv()
-                        back(t).wait_recv()
-                product(idx, 3, 2.0 * cells,
-                        [(own.at[q], lambda p: stat.at[p]), (sib.at[q], lambda p: stream.at[p])])
-
-            @pl.when(inner & (idx >= 4))
+                absorb_one(idx - LAG_ONE)
+
+            @pl.when(idx >= LAG_TWO)
             def _():
-                arriving = where(idx < 8, idx - 4, 4 + late(idx))
-                waits = (idx < 8) | (phase(idx) == 1)
-
-                @pl.when(waits)
-                def _():
-                    remote(own.at[0], stream.at[arriving], stream_send.at[arriving], stream_recv.at[arriving],
-                           (c, beyond)).wait_recv()
-                    product(idx, 2, 1.0 * cells, [(stream.at[arriving], lambda p: own.at[p])])
-
-                @pl.when(jnp.logical_not(waits))
-                def _():
-                    @pl.when(idx == 8)
-                    def _():
-                        for t in range(4):
-                            swap(t).wait_recv()
-                    held = where(phase(idx) == 0, late(idx), 4 + late(idx))
-                    product(idx, 2, 1.0 * cells, [(stream.at[held], lambda p: stat.at[p])])
-
-            fold_one(idx).start()
-
-            @pl.when(idx >= 1)
-            def _():
-                absorb_one(idx - 1)
-
-            @pl.when(idx >= 2)
-            def _():
-                absorb_two(idx - 2)
-
-        absorb_one(tasks - 1)
-        absorb_two(tasks - 2)
-        absorb_two(tasks - 1)
+                absorb_two(idx - LAG_TWO)
+
+    @pl.when(aux)
+    def _():
+        pl.loop(0, tasks)(deliver)
+
+    def store(r, piece):
+        down = pl.ds(pl.multiple_of(r * width, width), width)
+        along = pl.ds(pl.multiple_of(piece * width, width), width)
+        return pltpu.make_async_copy(result.at[r, piece], out_ref.at[down, along], store_done.at[r, piece])
 
     lanes[...] = jnp.zeros_like(lanes)
     height = 2 * width
@@ -351,10 +367,9 @@
     def _(n):
         piece = n // 2
         r = n % 2
-        mine = jnp.where(crossing, inner & (chip == piece),
-                         jnp.where(chip == g, chip == piece, outer & (chip == 2 * core + r)))
-
-        @pl.when(jnp.logical_not(mine & lead))
+        mine = (chip == piece) & (crossing | (chip == g) | inner)
+
+        @pl.when(jnp.logical_not(mine & aux))
         def _():
             remote(outn.at[0], inbox.at[side, r, piece], norm_send.at[0], in_recv.at[side, r, piece],
                    (other, g)).wait_recv()
@@ -364,6 +379,8 @@
             remote(outn.at[0], inbox.at[1 - side, r, piece], norm_send.at[0], in_recv.at[1 - side, r, piece],
                    (other, g)).wait_recv()
         total = inbox[0, r, piece].astype(jnp.int32) + inbox[1, r, piece].astype(jnp.int32)
+        result[r, piece] = total.astype(jnp.int16)
+        store(r, piece).start()
         value = total.astype(jnp.float32) * (1.0 / UNIT)
         square = value * value
         powered = square * square * square
@@ -371,7 +388,6 @@
         cols = g * block + piece * width + lax.broadcasted_iota(jnp.int32, (width, width), 1)
         powered = jnp.where(rows == cols, 0.0, powered)
         down = pl.ds(pl.multiple_of(r * width, width), width)
-        out_ref[down, pl.ds(pl.multiple_of(piece * width, width), width)] = powered
         part = powered[:, 0:128]
         for lane in range(1, width // 128):
             part = part + powered[:, lane * 128:(lane + 1) * 128]
@@ -383,7 +399,11 @@
     cin[g] = cmsg[...]
     for d in range(1, 4):
         conn_from(d).wait_recv()
-    conn_ref[...] = (cin[0] + cin[1]) + (cin[2] + cin[3])
+    conn_ref[...] = ((cin[0] + cin[1]) + (cin[2] + cin[3]))[0:1]
+
+    @pl.loop(0, 8)
+    def _(n):
+        store(n % 2, n // 2).wait()
 
     for d in range(1, 8):
         local_sums(d).wait_send()
@@ -399,18 +419,18 @@
     def _():
         for q in range(4):
             across(q).wait_send()
-            back(q).wait_send()
             relay(q).wait_send()
-
-    @pl.when(aux & outer)
-    def _():
-        for q in range(4):
-            inward(q).wait_send()
-
-    @pl.when(lead & inner)
+            beside(q).wait_send()
+
+    @pl.when(lead & outer)
     def _():
         for q in range(4):
             swap(q).wait_send()
+
+    @pl.when(lead & inner)
+    def _():
+        for t in range(8):
+            onward(t).wait_send()
 
     @pl.when(lead)
     def _():
@@ -418,62 +438,73 @@
         def _(idx):
             fold_one(idx).wait_send()
             fold_two(idx).wait_send()
-
+            hand(idx).wait_send()
+
+    @pl.when(aux)
+    def _():
+        @pl.loop(0, tasks)
+        def _(idx):
             @pl.when(jnp.logical_not(normal_here(idx)))
             def _():
                 normal(idx).wait_send()
 
-            @pl.when((rows_of(idx) != cols_of(idx)) & jnp.logical_not(turned_here(idx)))
+            @pl.when(idx >= 4)
             def _():
                 turned(idx).wait_send()
 
 
 def by_planes(counts, library):
-    factor = 10000.0 / library.astype(jnp.float32)
-    expressed = jnp.log1p(counts.astype(jnp.float32) * factor[:, None])
-    expressed = lax.reduce_precision(expressed, 8, 7)
-    cells, block = expressed.shape
+    cells, block = counts.shape
     width = block // QUARTERS
-    sums = jnp.stack([jnp.sum(expressed, axis=0), jnp.sum(expressed * expressed, axis=0)])
-    sums = jnp.concatenate([sums, jnp.zeros((6, block), jnp.float32)], axis=0)
-    own = expressed.astype(jnp.bfloat16).T.reshape(QUARTERS, width, cells)
+    slab = 128
     vmem = pl.BlockSpec(memory_space=pltpu.VMEM)
+    anywhere = pl.BlockSpec(memory_space=pl.ANY)
     dma = pltpu.SemaphoreType.DMA
     small = jnp.int16
-    count = 20
-    adjacency, connectivity = pl.pallas_call(
+    count = 16
+    quarters = pltpu.VMEM((QUARTERS, width, cells), jnp.bfloat16)
+    pieces = pltpu.VMEM((count, width, width), small)
+    row = pltpu.VMEM((8, block), jnp.float32)
+    totals, connectivity = pl.pallas_call(
         planes,
         out_shape=(
-            jax.ShapeDtypeStruct((2 * width, block), jnp.float32),
-            jax.ShapeDtypeStruct((8, 2 * width), jnp.float32),
+            jax.ShapeDtypeStruct((2 * width, block), small),
+            jax.ShapeDtypeStruct((1, 2 * width), jnp.float32),
         ),
-        in_specs=[vmem] * 2,
-        out_specs=(vmem, vmem),
+        in_specs=[anywhere, vmem],
+        out_specs=(anywhere, vmem),
         scratch_shapes=[
-            pltpu.VMEM((QUARTERS, width, cells), jnp.bfloat16),
-            pltpu.VMEM((QUARTERS, width, cells), jnp.bfloat16),
+            pltpu.VMEM((cells // slab, slab, block), jnp.int32),
+            quarters, row, row,
+            pltpu.VMEM((2, 4, width, width), small),
+            quarters, quarters, quarters,
             pltpu.VMEM((8, width, cells), jnp.bfloat16),
             pltpu.VMEM((count, 4, width, width), small),
             pltpu.VMEM((count, 2, width, width), small),
-            pltpu.VMEM((count, width, width), small),
-            pltpu.VMEM((count, width, width), small),
-            pltpu.VMEM((count, width, width), small),
+            pieces, pieces, pieces, pieces,
             pltpu.VMEM((2, 2, 4, width, width), small),
             pltpu.VMEM((8, 8, block), jnp.float32),
-            pltpu.VMEM((8, block), jnp.float32),
+            row,
             pltpu.VMEM((4, 8, block), jnp.float32),
             pltpu.VMEM((4, block, 8), jnp.float32),
             pltpu.VMEM((2 * width, 128), jnp.float32),
             pltpu.VMEM((8, 2 * width), jnp.float32),
             pltpu.VMEM((4, 8, 2 * width), jnp.float32),
-            dma((4,)), dma((4,)), dma((4,)), dma, dma, dma((8,)), dma((8,)), pltpu.SemaphoreType.REGULAR,
-            dma((count,)), dma((count,)), dma((count,)), dma((count,)), dma((count,)), dma((count,)), dma((2, 2, 4)),
+            dma((4,)), dma((4,)), dma((4,)), dma((4,)), dma, dma, dma((8,)), dma((8,)), pltpu.SemaphoreType.REGULAR,
+            dma((count,)), dma((count,)), dma((count,)), dma((count,)), dma((count,)), dma((count,)),
+            dma((count,)), dma((count,)), dma((2, 2, 4)),
+            dma((cells // slab,)), dma((2, 4)),
             dma((8,)), dma((8,)), dma((4,)), dma((4,)), dma((4,)), dma((4,)),
         ],
         compiler_params=pltpu.CompilerParams(
             collective_id=1, has_side_effects=True, vmem_limit_bytes=58 * 1024 * 1024),
-    )(own, sums)
-    return adjacency, connectivity[0]
+    )(counts, library.reshape(cells // slab, slab))
+    value = totals.astype(jnp.float32) * (1.0 / UNIT)
+    square = value * value
+    rows = lax.axis_index("cells") * 2 * width + jnp.arange(2 * width, dtype=jnp.int32)[:, None]
+    cols = lax.axis_index("genes") * block + jnp.arange(block, dtype=jnp.int32)[None, :]
+    adjacency = jnp.where(rows == cols, jnp.float32(0.0), square * square * square)
+    return adjacency, connectivity.reshape(2 * width)
 
 
 def network(cell_groups, gene_groups, xq_ref, own_ref, sums_ref, out_ref, stats_ref,
@@ -698,8 +729,15 @@
 
 def solution(mesh):
     sized = mesh.shape["genes"] == 4 and mesh.shape["cells"] == 8
+
+    def body(counts, library):
+        cells, block = counts.shape
+        if sized and cells % 1024 == 0 and block % 512 == 0:
+            return by_planes(counts, library)
+        return shards(counts, library)
+
     return jax.shard_map(
-        by_planes if sized else shards,
+        body,
         mesh=mesh,
         in_specs=(P("cells", "genes"), P("cells")),
         out_specs=(P("cells", "genes"), P("cells")),

time: 155 us -> 112 us (0.72)
  Pallas kernels: 141 us -> 108 us
  local copies, waits for them, and re-layouts: 7.07 us -> 0.58 us
  other arithmetic: 5.75 us -> 3.23 us
    pallas_call x1, Pallas kernels: 141 us -> 108 us  [by_planes(): pl.pallas_call(planes, out_shape=(jax.ShapeDtypeStruct((2 * width, block)...]
    reduce_sum x1 -> x0, other arithmetic: 4.39 us -> none  [by_planes(): jnp.sum(expressed, axis=0)]
    select_n x0 -> x1, other arithmetic: none -> 3.22 us  [by_planes(): jnp.where(rows == cols, jnp.float32(0.0), square * square * square)]
    unnamed x1 -> x3, local copies, waits for them, and re-layouts: 3.16 us -> 0.58 us
    transpose x1 -> x0, local copies, waits for them, and re-layouts: 2.54 us -> none  [by_planes(): own = expressed.astype(jnp.bfloat16).T.reshape(QUARTERS, width, cells)]
where the time goes in v1:
time: 112 us
  Pallas kernels  108 us (96%)
  other arithmetic  3.23 us (3%)
    pallas_call x1, Pallas kernels, by_planes(): pl.pallas_call(planes, out_shape=(jax.ShapeDtypeStruct((2 * width, block)...  108 us
    select_n x1, other arithmetic, by_planes(): jnp.where(rows == cols, jnp.float32(0.0), square * square * square)  3.22 us

profile of v1, /device:TPU:1, one launch (start us, length us, event | category | flops | bytes accessed | tf_op | source)
XLA Modules:
  0.0 112.2 jit_solution(12002186866945148454)
XLA Ops:
  0.7 107.7 %shard_map.41 = (s16[512,1024]{1,0:T(8,128)(2,1)}, f32[1,512]{1,0:T(1,128)}) custom-call(s32[1024,1024]{1,0:T(8,128)} %counts_ref.1, s32[8,128]{1,0:T(8,128)} %bitcast.2), custom_call_target="tpu_custom_call" | custom-call | tf_op jit(solution)/shard_map/pallas_call | solution.py:468
  108.4 0.0 copy-start
  108.4 3.2 %fusion = f32[512,1024]{1,0:T(8,128)} fusion(s16[512,1024]{1,0:T(8,128)(2,1)} %get-tuple-element.4, s32[1024]{0:T(1024)S(1)} %iota_add_fusion, s32[512]{0:T(512)S(1)} %iota_add_fusion.1), kind=kLoop, calls=%fused_computation.1 | loop fusion | flops 3670016 | bytes 3151872 | tf_op jit(solution)/shard_map/jit(_where)/select_n | solution.py:506
  111.6 0.0 copy-done
  111.6 0.6 copy.5
  (2 shorter events, 0.0 us)
Async XLA Ops:
  108.4 3.2 %copy-start = (f32[1,512]{1,0:T(1,128)S(1)}, f32[1,512]{1,0:T(1,128)}, u32[]{:S(2)}) copy-start(f32[1,512]{1,0:T(1,128)} %get-tuple-element.5) | copy-start | bytes 6148

commit v2 on v1

--- a/solution.py
+++ b/solution.py
@@ -11,8 +11,9 @@
 TILE = 512
 QUARTERS = 4
 UNIT = 28000.0
-LAG_ONE = 3
-LAG_TWO = 5
+FOLDED = tuple(min(16, max(0, n - 1)) for n in range(20))
+SUMMED = tuple(min(16, max(0, n - 3)) for n in range(20))
+NEAR_ORDER = (0, 1, 2, 3, 4, 5, 6, 7, 8, 9, 10, 12, 11, 13, 14, 15)
 GO_AT = 6
 MESH = pl.DeviceIdType.MESH
 
@@ -28,7 +29,7 @@
 def planes(counts_ref, library_ref, out_ref, conn_ref,
            raw, own, sums_ref, squares, result, sib, stat, held, stream, tiles, land1, land2, whole, outn, outt, inbox,
            pstat, message, table, columns, lanes, cmsg, cin,
-           stat_send, stat_recv, held_send, held_recv, sib_send, sib_recv, stream_send, stream_recv, go,
+           stat_send, stat_recv, held_send, held_recv, sib_send, sib_recv, stream_send, stream_recv, pass_send, onward_send, go,
            one_send, one_recv, two_send, two_recv, hand_send, hand_recv, norm_send, turn_send, in_recv,
            load_done, store_done, sum_send, sum_recv, row_send, row_recv, conn_send, conn_recv):
     quarters, width, cells = own.shape
@@ -92,19 +93,22 @@
         return remote(own, sib, sib_send, sib_recv, (other, g))
 
     def across(q):
-        return remote(own.at[q], stream.at[q], stream_send.at[q], stream_recv.at[q], (c, beyond))
+        return remote(own.at[q], stream.at[q], stream_send.at[q], stream_recv.at[q], (other, beyond))
 
     def inward(q):
-        return remote(own.at[q], stream.at[4 + q], stream_send.at[q], stream_recv.at[4 + q], (c, near))
+        return remote(own.at[q], held.at[q], stream_send.at[q], held_recv.at[q], (c, near))
 
     def relay(q):
-        return remote(stream.at[4 + q], stream.at[4 + q], stream_send.at[4 + q], stream_recv.at[4 + q], (c, beyond))
+        return remote(held.at[q], stream.at[4 + q], stream_send.at[4 + q], stream_recv.at[4 + q], (other, beyond))
 
     def beside(q):
-        return remote(stream.at[4 + q], held.at[q], held_send.at[q], held_recv.at[q], (other, g))
+        return remote(held.at[q], held.at[q], held_send.at[q], held_recv.at[q], (other, g))
+
+    def passed(t):
+        return remote(stream.at[t], stream.at[t], pass_send.at[t], stream_recv.at[t], (other, g))
 
     def onward(t):
-        return remote(stream.at[t], stream.at[t], stream_send.at[t], stream_recv.at[t], (c, far))
+        return remote(stream.at[t], stream.at[t], onward_send.at[t], stream_recv.at[t], (other, far))
 
     def swap(q):
         return remote(own.at[q], stat.at[q], stat_send.at[q], stat_recv.at[q], (c, near))
@@ -180,6 +184,13 @@
             inward(q).wait_recv()
             relay(q).start()
             beside(q).start()
+            across(q).wait_recv()
+            passed(q).start()
+            onward(q).start()
+        for q in range(4):
+            relay(q).wait_recv()
+            passed(4 + q).start()
+            onward(4 + q).start()
 
     @pl.when(aux & outer)
     def _():
@@ -218,6 +229,20 @@
         return remote(tiles.at[idx, 1], land2.at[idx], two_send.at[idx], two_recv.at[idx],
                       (2 * partner + core, g))
 
+    def task_at(n):
+        code = 0
+        for index, near_task in enumerate(NEAR_ORDER):
+            code = where(n == index, where(inner, near_task, index), code)
+        return code
+
+    def reached(table, n):
+        value = 0
+        for index, entry in enumerate(table):
+            value = where(n == index, entry, value)
+        return jnp.minimum(value, tasks)
+
+    tasks = where(inner, 16, 12)
+
     def rows_of(idx):
         crossed = where(idx < 8, beyond, where(idx < 12, farther, far))
         return where(idx < 4, g, crossed)
@@ -227,7 +252,7 @@
 
     def normal(idx):
         q = idx % 4
-        return remote(outn.at[idx], inbox.at[side, q % 2, chip], norm_send.at[idx], in_recv.at[side, q % 2, chip],
+        return remote(whole.at[idx], inbox.at[side, q % 2, chip], norm_send.at[idx], in_recv.at[side, q % 2, chip],
                       (2 * rows_of(idx) + q // 2, g))
 
     def turned(idx):
@@ -248,25 +273,24 @@
         total = (tiles[idx, 0].astype(jnp.int32) + land1[idx, 0].astype(jnp.int32)
                  + land2[idx].astype(jnp.int32))
         whole[idx] = total.astype(jnp.int16)
-        hand(idx).start()
+
+        @pl.when(idx >= 4)
+        def _():
+            hand(idx).start()
+        here = normal_here(idx)
+
+        @pl.when(here)
+        def _():
+            inbox[side, (idx % 4) % 2, chip] = total.astype(jnp.int16)
+
+        @pl.when(jnp.logical_not(here))
+        def _():
+            normal(idx).start()
 
     def deliver(idx):
         hand(idx).wait_recv()
-        q = idx % 4
-        here = normal_here(idx)
-
-        @pl.when(here)
-        def _():
-            inbox[side, q % 2, chip] = outn[idx]
-
-        @pl.when(jnp.logical_not(here))
-        def _():
-            normal(idx).start()
-
-        @pl.when(idx >= 4)
-        def _():
-            outt[idx] = jnp.transpose(outn[idx].astype(jnp.int32)).astype(jnp.int16)
-            turned(idx).start()
+        outt[idx] = jnp.transpose(outn[idx].astype(jnp.int32)).astype(jnp.int16)
+        turned(idx).start()
 
     def product(idx, row, count, parts):
         row_block = rows_of(idx)
@@ -290,8 +314,6 @@
             value = (acc * scale_j - mean_j * drift_i - sum_j * mean_i) * scale_i
             tiles[idx, place(p, idx)] = jnp.round(value).astype(jnp.int32).astype(jnp.int16)
 
-    tasks = where(inner, 16, 12)
-
     def step(idx):
         q = idx % 4
 
@@ -316,11 +338,7 @@
         @pl.when((idx >= 4) & (idx < 12))
         def _():
             slot = idx - 4
-            remote(own.at[0], stream.at[slot], stream_send.at[slot], stream_recv.at[slot], (c, beyond)).wait_recv()
-
-            @pl.when(inner)
-            def _():
-                onward(slot).start()
+            passed(slot).wait_recv()
             product(idx, 2, 1.0 * cells, [(stream.at[slot], lambda p: own.at[p])])
 
         @pl.when(idx >= 12)
@@ -337,23 +355,25 @@
         columns[g] = jnp.transpose(table[g])
         share().wait_recv()
 
-        @pl.loop(0, tasks + LAG_TWO)
-        def _(idx):
-            @pl.when(idx < tasks)
+        @pl.loop(0, len(FOLDED))
+        def _(n):
+            @pl.when(n < tasks)
             def _():
-                step(idx)
-
-            @pl.when((idx >= LAG_ONE) & (idx < tasks + LAG_ONE))
-            def _():
-                absorb_one(idx - LAG_ONE)
-
-            @pl.when(idx >= LAG_TWO)
-            def _():
-                absorb_two(idx - LAG_TWO)
+                step(task_at(n))
+
+            @pl.loop(reached(FOLDED, n - 1), reached(FOLDED, n))
+            def _(m):
+                absorb_one(task_at(m))
+
+            @pl.loop(reached(SUMMED, n - 1), reached(SUMMED, n))
+            def _(m):
+                absorb_two(task_at(m))
 
     @pl.when(aux)
     def _():
-        pl.loop(0, tasks)(deliver)
+        @pl.loop(4, tasks)
+        def _(n):
+            deliver(task_at(n))
 
     def store(r, piece):
         down = pl.ds(pl.multiple_of(r * width, width), width)
@@ -369,7 +389,7 @@
         r = n % 2
         mine = (chip == piece) & (crossing | (chip == g) | inner)
 
-        @pl.when(jnp.logical_not(mine & aux))
+        @pl.when(jnp.logical_not(mine & lead))
         def _():
             remote(outn.at[0], inbox.at[side, r, piece], norm_send.at[0], in_recv.at[side, r, piece],
                    (other, g)).wait_recv()
@@ -396,6 +416,51 @@
     cmsg[...] = jnp.broadcast_to(jnp.sum(jnp.transpose(lanes[...]), axis=0, keepdims=True), cmsg.shape)
     for d in range(1, 4):
         conn_to(d).start()
+    for d in range(1, 8):
+        local_sums(d).wait_send()
+    for d in range(1, 4):
+        genes_to(d).wait_send()
+
+    @pl.when(aux)
+    def _():
+        share().wait_send()
+
+    @pl.when(aux & inner)
+    def _():
+        for q in range(4):
+            across(q).wait_send()
+            relay(q).wait_send()
+            beside(q).wait_send()
+        for t in range(8):
+            passed(t).wait_send()
+            onward(t).wait_send()
+
+    @pl.when(lead & outer)
+    def _():
+        for q in range(4):
+            swap(q).wait_send()
+
+    @pl.when(lead)
+    def _():
+        @pl.loop(0, tasks)
+        def _(idx):
+            fold_one(idx).wait_send()
+            fold_two(idx).wait_send()
+
+            @pl.when(idx >= 4)
+            def _():
+                hand(idx).wait_send()
+
+            @pl.when(jnp.logical_not(normal_here(idx)))
+            def _():
+                normal(idx).wait_send()
+
+    @pl.when(aux)
+    def _():
+        @pl.loop(4, tasks)
+        def _(idx):
+            turned(idx).wait_send()
+
     cin[g] = cmsg[...]
     for d in range(1, 4):
         conn_from(d).wait_recv()
@@ -404,53 +469,8 @@
     @pl.loop(0, 8)
     def _(n):
         store(n % 2, n // 2).wait()
-
-    for d in range(1, 8):
-        local_sums(d).wait_send()
     for d in range(1, 4):
-        genes_to(d).wait_send()
         conn_to(d).wait_send()
-
-    @pl.when(aux)
-    def _():
-        share().wait_send()
-
-    @pl.when(aux & inner)
-    def _():
-        for q in range(4):
-            across(q).wait_send()
-            relay(q).wait_send()
-            beside(q).wait_send()
-
-    @pl.when(lead & outer)
-    def _():
-        for q in range(4):
-            swap(q).wait_send()
-
-    @pl.when(lead & inner)
-    def _():
-        for t in range(8):
-            onward(t).wait_send()
-
-    @pl.when(lead)
-    def _():
-        @pl.loop(0, tasks)
-        def _(idx):
-            fold_one(idx).wait_send()
-            fold_two(idx).wait_send()
-            hand(idx).wait_send()
-
-    @pl.when(aux)
-    def _():
-        @pl.loop(0, tasks)
-        def _(idx):
-            @pl.when(jnp.logical_not(normal_here(idx)))
-            def _():
-                normal(idx).wait_send()
-
-            @pl.when(idx >= 4)
-            def _():
-                turned(idx).wait_send()
 
 
 def by_planes(counts, library):
@@ -490,7 +510,7 @@
             pltpu.VMEM((2 * width, 128), jnp.float32),
             pltpu.VMEM((8, 2 * width), jnp.float32),
             pltpu.VMEM((4, 8, 2 * width), jnp.float32),
-            dma((4,)), dma((4,)), dma((4,)), dma((4,)), dma, dma, dma((8,)), dma((8,)), pltpu.SemaphoreType.REGULAR,
+            dma((4,)), dma((4,)), dma((4,)), dma((4,)), dma, dma, dma((8,)), dma((8,)), dma((8,)), dma((8,)), pltpu.SemaphoreType.REGULAR,
             dma((count,)), dma((count,)), dma((count,)), dma((count,)), dma((count,)), dma((count,)),
             dma((count,)), dma((count,)), dma((2, 2, 4)),
             dma((cells // slab,)), dma((2, 4)),

time: 112 us -> 110 us (0.982)
  Pallas kernels: 108 us -> 105 us
    pallas_call x1, Pallas kernels: 108 us -> 105 us  [by_planes(): pl.pallas_call(planes, out_shape=(jax.ShapeDtypeStruct((2 * width, block)...]
where the time goes in v2:
time: 110 us
  Pallas kernels  105 us (95%)
  other arithmetic  3.23 us (3%)
    pallas_call x1, Pallas kernels, by_planes(): pl.pallas_call(planes, out_shape=(jax.ShapeDtypeStruct((2 * width, block)...  105 us
    select_n x1, other arithmetic, by_planes(): jnp.where(rows == cols, jnp.float32(0.0), square * square * square)  3.22 us

profile of v2, /device:TPU:1, one launch (start us, length us, event | category | flops | bytes accessed | tf_op | source)
XLA Modules:
  0.0 109.9 jit_solution(4406203402313355064)
XLA Ops:
  0.7 105.4 %shard_map.41 = (s16[512,1024]{1,0:T(8,128)(2,1)}, f32[1,512]{1,0:T(1,128)}) custom-call(s32[1024,1024]{1,0:T(8,128)} %counts_ref.1, s32[8,128]{1,0:T(8,128)} %bitcast.2), custom_call_target="tpu_custom_call" | custom-call | tf_op jit(solution)/shard_map/pallas_call | solution.py:488
  106.1 0.0 copy-start
  106.1 3.2 %fusion = f32[512,1024]{1,0:T(8,128)} fusion(s16[512,1024]{1,0:T(8,128)(2,1)} %get-tuple-element.4, s32[1024]{0:T(1024)S(1)} %iota_add_fusion, s32[512]{0:T(512)S(1)} %iota_add_fusion.1), kind=kLoop, calls=%fused_computation.1 | loop fusion | flops 3670016 | bytes 3151872 | tf_op jit(solution)/shard_map/jit(_where)/select_n | solution.py:526
  109.3 0.0 copy-done
  109.3 0.6 copy.5
  (2 shorter events, 0.0 us)
Async XLA Ops:
  106.1 3.2 %copy-start = (f32[1,512]{1,0:T(1,128)S(1)}, f32[1,512]{1,0:T(1,128)}, u32[]{:S(2)}) copy-start(f32[1,512]{1,0:T(1,128)} %get-tuple-element.5) | copy-start | bytes 6148

commit v3 on v2

--- a/solution.py
+++ b/solution.py
@@ -120,12 +120,11 @@
         source = lax.rem(c + d, 8)
         return remote(sums_ref, pstat.at[source], sum_send.at[d], sum_recv.at[source], (source, g))
 
-    def genes_to(d):
-        return remote(message, table.at[g], row_send.at[d], row_recv.at[g], (c, lax.rem(g + d, 4)))
-
-    def genes_from(d):
-        source = lax.rem(g + d, 4)
-        return remote(message, table.at[source], row_send.at[d], row_recv.at[source], (c, source))
+    def genes_to(z):
+        return remote(message, table.at[g], row_send.at[z], row_recv.at[g], (c, z))
+
+    def genes_from(z):
+        return remote(message, table.at[z], row_send.at[z], row_recv.at[z], (c, z))
 
     def conn_to(d):
         return remote(cmsg, cin.at[g], conn_send.at[d], conn_recv.at[g], (c, lax.rem(g + d, 4)))
@@ -173,8 +172,16 @@
     message[3:4] = together[0:1]
     message[4:8] = jnp.zeros((4, block), jnp.float32)
     table[g] = message[...]
-    for d in range(1, 4):
-        genes_to(d).start()
+    pair = g + 1 - 2 * (g % 2)
+
+    @pl.when(lead)
+    def _():
+        genes_to(pair).start()
+
+    @pl.when(aux)
+    def _():
+        genes_to(beyond).start()
+        genes_to(farther).start()
 
     @pl.when(aux & inner)
     def _():
@@ -200,10 +207,6 @@
             inward(q).wait_send()
         pl.semaphore_signal(go, inc=1, device_id=(other, g), device_id_type=MESH)
 
-    @pl.when(aux)
-    def _():
-        for d in range(1, 4):
-            genes_from(d).wait_recv()
 
     def where(test, yes, no):
         return jnp.where(test, yes, no)
@@ -319,9 +322,8 @@
 
         @pl.when(idx == 4)
         def _():
-            for d in range(1, 4):
-                genes_from(d).wait_recv()
-                z = lax.rem(g + d, 4)
+            for z in (pair, beyond, farther):
+                genes_from(z).wait_recv()
                 columns[z] = jnp.transpose(table[z])
 
         @pl.when(outer & (idx == GO_AT))
@@ -418,8 +420,14 @@
         conn_to(d).start()
     for d in range(1, 8):
         local_sums(d).wait_send()
-    for d in range(1, 4):
-        genes_to(d).wait_send()
+    @pl.when(lead)
+    def _():
+        genes_to(pair).wait_send()
+
+    @pl.when(aux)
+    def _():
+        genes_to(beyond).wait_send()
+        genes_to(farther).wait_send()
 
     @pl.when(aux)
     def _():

time: 110 us -> 109 us (level)
    pallas_call x1, Pallas kernels: 105 us -> 104 us  [by_planes(): pl.pallas_call(planes, out_shape=(jax.ShapeDtypeStruct((2 * width, block)...]
where the time goes in v3:
time: 109 us
  Pallas kernels  104 us (95%)
  other arithmetic  3.23 us (3%)
    pallas_call x1, Pallas kernels, by_planes(): pl.pallas_call(planes, out_shape=(jax.ShapeDtypeStruct((2 * width, block)...  104 us
    select_n x1, other arithmetic, by_planes(): jnp.where(rows == cols, jnp.float32(0.0), square * square * square)  3.22 us

profile of v3, /device:TPU:1, one launch (start us, length us, event | category | flops | bytes accessed | tf_op | source)
XLA Modules:
  0.0 108.5 jit_solution(15981040097515377685)
XLA Ops:
  0.7 104.0 %shard_map.41 = (s16[512,1024]{1,0:T(8,128)(2,1)}, f32[1,512]{1,0:T(1,128)}) custom-call(s32[1024,1024]{1,0:T(8,128)} %counts_ref.1, s32[8,128]{1,0:T(8,128)} %bitcast.2), custom_call_target="tpu_custom_call" | custom-call | tf_op jit(solution)/shard_map/pallas_call | solution.py:496
  104.7 0.0 copy-start
  104.7 3.2 %fusion = f32[512,1024]{1,0:T(8,128)} fusion(s16[512,1024]{1,0:T(8,128)(2,1)} %get-tuple-element.4, s32[1024]{0:T(1024)S(1)} %iota_add_fusion, s32[512]{0:T(512)S(1)} %iota_add_fusion.1), kind=kLoop, calls=%fused_computation.1 | loop fusion | flops 3670016 | bytes 3151872 | tf_op jit(solution)/shard_map/jit(_where)/select_n | solution.py:534
  107.9 0.0 copy-done
  108.0 0.6 copy.5
  (2 shorter events, 0.0 us)
Async XLA Ops:
  104.7 3.2 %copy-start = (f32[1,512]{1,0:T(1,128)S(1)}, f32[1,512]{1,0:T(1,128)}, u32[]{:S(2)}) copy-start(f32[1,512]{1,0:T(1,128)} %get-tuple-element.5) | copy-start | bytes 6148
